TPU v7x, 512 devices: a whole 4x8x8 slice. The times are simulated.
512 devices in a mesh: va: 16 (over z_hi, y), vb: 8 (over z_lo, core), occ: 4 (over x).
Axes of the slice: x: 4, y: 8, z: 8 (z_hi: 2, z_lo: 4; z = z_hi * 4 + z_lo), core: 2. Of those that a mesh axis runs over, the one named last changes fastest.
Arguments:
- amplitudes: bfloat16 [6, 1536, 1536], P(None, 'va', 'occ'), may hold values from -6 to 6
- bra_factor: bfloat16 [16, 1536, 1536], P('vb', 'va'), may hold values from -0.078125 to 0.078125
- ket_factor: bfloat16 [16, 1536, 1536], P('va', ('vb', 'occ')), may hold values from -0.15625 to 0.15625
- pair_list: int32 [8, 4], replicated, may hold values from 0 to 5, as said below
Outputs:
- ladder: float32 [6, 1536, 1536], P(None, 'va', ('vb', 'occ'))
Inputs may be any that keep to these rules, and one draw needn't show every extreme that they name: `pair_list`: each row names 4 different pairs, and every pair of 0 to 5 is named by some row.
All inputs are finite; a program needn't handle non-finite values.
Results may differ from a plain program's by a relative error of at most 0.0042.
Values may be sent and summed in bfloat16 or wider, within the bound.
No kernel may reach another device: no remote copies, remote signals or barrier semaphores. Data moves between devices by JAX's collectives and lax.ppermute only.
A program may use at most 64 MiB of HBM per device.

v0:
```python
import functools

import jax
import jax.numpy as jnp
from jax import lax
from jax.experimental import pallas as pl
from jax.experimental.pallas import tpu as pltpu
from jax.sharding import Mesh
from jax.sharding import PartitionSpec as P

AXES = ("zh", "y", "zl", "core", "x")
VA = ("zh", "y")
F32 = jnp.float32
BF16 = jnp.bfloat16
VMEM = pl.BlockSpec(memory_space=pltpu.VMEM)
SMEM = pl.BlockSpec(memory_space=pltpu.SMEM)
PARAMS = pltpu.CompilerParams(vmem_limit_bytes=16 << 20)


def shifted(block, axis, by):
    n = lax.axis_size(axis)
    return lax.ppermute(block, axis, [(i, (i + by) % n) for i in range(n)])


def both_ways(block):
    n = lax.axis_size("x")
    route = [(n * c + i, n * c + (i + 1 - 2 * c) % n) for i in range(n) for c in range(2)]
    return lax.ppermute(block, ("core", "x"), route)


def copies_from(array, axis):
    copies = jnp.broadcast_to(array, (lax.axis_size(axis), *array.shape))
    return lax.all_to_all(copies, axis, 0, 0, tiled=True)


def position(name):
    return lax.axis_index(name).astype(jnp.int32)


def half_kernel(steps, lists, *refs):
    kets, refs = refs[: len(steps)], refs[len(steps) :]
    own, near, near_other, far, far_other = refs[:5]
    half = refs[-1]
    zh, y, _, core, x = [position(name) for name in AXES]
    n_own, rows, width = far.shape
    cols = kets[0].shape[1]
    step = 1 - 2 * core
    firsts = [n_own * core, n_own * (1 - core)]
    chunks = [(x, [own[pl.ds(f, n_own)] for f in firsts])]
    chunks.append((x - step, [near[pl.ds(f, n_own)] for f in firsts]))
    chunks.append((x + step, [near_other[pl.ds(f, n_own)] for f in firsts]))
    chunks.append((x + 2, [far[...], far_other[...]]))
    out = None
    for place, taus in chunks:
        at = pl.multiple_of(((place + 4) % 4) * width, 128)
        lhs = jnp.concatenate([ket[h, :, pl.ds(at, width)] for ket in kets for h in range(2)], axis=0)
        rhs = jnp.concatenate(taus, axis=0).reshape(2 * n_own * rows, width)
        term = lax.dot_general(lhs, rhs, (((1,), (1,)), ((), ())), preferred_element_type=F32)
        out = term if out is None else out + term
    if len(refs) > 6:
        for d in set(range(8)) - set(steps):
            half[2 * d : 2 * d + 2] = refs[5][2 * d : 2 * d + 2]
    for n, d in enumerate(steps):
        for h in range(2):
            high = zh if h == 0 else 1 - zh
            group = (8 * high + (y - d + 8) % 8) // 2
            i = 2 * n + h
            for side in range(2):
                for k in range(n_own):
                    p = firsts[side] + k
                    at = (side * n_own + k) * rows
                    wanted = lists[0, group] == p
                    for m in range(1, lists.shape[0]):
                        wanted = jnp.logical_or(wanted, lists[m, group] == p)
                    block = out[i * cols : (i + 1) * cols, at : at + rows]
                    block = jnp.where(wanted, block, 0.0).astype(BF16)
                    half[2 * d + h, pl.ds(pl.multiple_of(p * cols, 16), cols), :] = block


def half_of(steps, lists, kets, taus, before):
    pairs, rows, _ = taus[0].shape
    _, cols, _ = kets[0].shape
    earlier = [] if before is None else [before]
    operands = [kets[d] for d in steps] + taus + earlier
    return pl.pallas_call(
        functools.partial(half_kernel, steps),
        in_specs=[SMEM] + [VMEM] * len(operands),
        out_specs=VMEM,
        out_shape=jax.ShapeDtypeStruct((2 * len(kets), pairs * cols, rows), BF16),
        compiler_params=PARAMS,
    )(lists, *operands)


def total_kernel(half, mine, theirs, out, lhs):
    parts, places, blocks, rows, width = mine.shape
    zh, y, _, core, _ = [position(name) for name in AXES]
    m = half.shape[1]
    keep = m * rows // 128
    n = 0
    for r in range(2):
        side = core if r == 0 else 1 - core
        for z in range(places):
            for j in range(blocks):
                q = places * z + blocks * side + j
                slot = 2 * ((y - q % 8 + 8) % 8) + jnp.where(q // 8 == zh, 0, 1)
                lhs[:, n : n + rows] = half[slot]
                n += rows
    n_c = places * blocks * rows
    for x in range(parts):
        sums = 0.0
        for side, ref in enumerate((mine, theirs)):
            rhs = ref[x].reshape(n_c, width)
            sums = sums + jnp.dot(lhs[:, side * n_c : (side + 1) * n_c], rhs, preferred_element_type=F32)
        for i in range(width // rows):
            block = sums[:, i * rows : (i + 1) * rows]
            tail = jnp.concatenate([block[keep:, 32 * s : 32 * s + 32] for s in range(rows // 32)], axis=0)
            va = x * (width // rows) + i
            out[va % 8 * 2 + va // 8] = jnp.concatenate([block[:keep], tail], axis=1).astype(BF16)


def sum_kernel(parts, out):
    rows = out.shape[1]
    keep, step = parts.shape[1], out.shape[0] - parts.shape[1]
    sums = parts[0].astype(F32)
    for i in range(1, parts.shape[0]):
        sums = sums + parts[i].astype(F32)
    out[:keep, :] = sums[:, :rows]
    tail = [sums[step * s : step * (s + 1), rows:] for s in range(rows // 32)]
    out[keep:, :] = jnp.concatenate(tail, axis=1)


def per_device(amplitudes, bra_factor, ket_factor, pair_list):
    pairs, rows, _ = amplitudes.shape
    cols = ket_factor.shape[1]
    n_a = bra_factor.shape[2]
    core = lax.axis_index("core")
    n_own = n_a // lax.axis_size("x")

    ket = jnp.concatenate([ket_factor, shifted(ket_factor, "zh", 1)], axis=0)
    ahead, behind = [ket], [ket]
    for s in range(1, 5):
        ahead.append(shifted(ahead[-1], "y", 1))
        if s < 4:
            behind.append(shifted(behind[-1], "y", -1))
    kets = ahead + behind[:0:-1]
    own = lax.dynamic_slice_in_dim(bra_factor, n_own * lax.axis_index("x"), n_own, 2)
    bra = copies_from(copies_from(own, "zl"), "x")
    near = both_ways(amplitudes)
    far = lax.dynamic_slice_in_dim(amplitudes, core * (pairs // 2), pairs // 2, 0)
    far = shifted(far, "x", 2)
    taus = [amplitudes, near, shifted(near, "core", 1), far, shifted(far, "core", 1)]
    bra_other = shifted(bra, "core", 1)

    half = half_of((0, 1, 2, 6, 7), pair_list.T, kets, taus, None)
    half = half_of((3, 4, 5), pair_list.T, kets, taus, half)
    n_va = n_a // rows
    total = pl.pallas_call(
        total_kernel,
        in_specs=[VMEM] * 3,
        out_specs=VMEM,
        out_shape=jax.ShapeDtypeStruct((n_va, pairs * cols * rows // 128, 128), BF16),
        scratch_shapes=[pltpu.VMEM((pairs * cols, half.shape[0] * rows), BF16)],
        compiler_params=PARAMS,
        name="total",
    )(half, bra, bra_other)
    total = lax.all_to_all(total, ("y", "zh"), 0, 0, tiled=True)
    out = pl.pallas_call(
        sum_kernel,
        in_specs=[VMEM],
        out_specs=VMEM,
        out_shape=jax.ShapeDtypeStruct((pairs * cols, rows), F32),
        compiler_params=PARAMS,
        name="sum",
    )(total)
    return out.reshape(pairs, cols, rows).transpose(0, 2, 1)


def solution(mesh):
    torus = Mesh(mesh.devices.reshape(2, 8, 4, 2, 4), AXES)
    return jax.shard_map(
        per_device,
        mesh=torus,
        in_specs=(P(None, VA, "x"), P(("zl", "core"), VA, None), P(VA, ("zl", "core", "x"), None), P()),
        out_specs=P(None, VA, ("zl", "core", "x")),
        check_vma=False,
    )
```

profile of v0, /device:TPU:64, one launch (start us, length us, event | category | flops | bytes accessed | tf_op | source)
XLA Modules:
  0.0 167.4 jit_solution(15213915833726587235)
XLA Ops:
  0.0 1.1 copy-done
  1.1 21.0 %all_to_all.15 = bf16[4,2,96,384]{3,2,1,0:T(8,128)(2,1)S(1)} all-to-all(bf16[4,2,96,384]{3,2,1,0:T(8,128)(2,1)S(1)} %broadcast_in_dim.6), channel_id=1, replica_groups=mesh['zh'=2,'y'=8,'zl'=4,'core'=2,'x'=4] {'zl'}, dimensions={0} | all-to-all | bytes 1179648 | tf_op jit(solution)/shard_map/all_to_all | solution.py:33
  22.1 0.3 broadcast_in_dim.7
  22.5 32.1 %all_to_all.16.mine = bf16[4,4,2,96,384]{4,3,2,1,0:T(8,128)(2,1)S(1)} all-to-all(bf16[4,4,2,96,384]{4,3,2,1,0:T(8,128)(2,1)S(1)} %broadcast_in_dim.7), channel_id=1, replica_groups=mesh['zh'=2,'y'=8,'zl'=4,'core'=2,'x'=4] {'x'}, dimensions={0} | all-to-all | bytes 4718592 | tf_op jit(solution)/shard_map/all_to_all | solution.py:33
  54.6 1.9 %collective-permute-start.12 = (bf16[4,4,2,96,384]{4,3,2,1,0:T(8,128)(2,1)S(1)}, bf16[4,4,2,96,384]{4,3,2,1,0:T(8,128)(2,1)}, u32[]{:S(2)}, u32[]{:S(2)}) collective-permute-start(bf16[4,4,2,96,384]{4,3,2,1,0:T(8,128)(2,1)S(1)} %all_to_all.16.mine), channel_id=1, source_target_pairs={{0,4},{4,0},{1,5},{5,1},{2,6},{6,2},{3,7},{7,3},{8,12},{12,8},{9,1... | collective-permute-start | bytes 7077896 | tf_op jit(solution)/shard_map/ppermute | solution.py:22
  56.5 8.2 %collective-permute-start = (bf16[1,48,1536]{2,1,0:T(8,128)(2,1)S(1)}, bf16[1,48,1536]{2,1,0:T(8,128)(2,1)S(1)}, u32[]{:S(2)}, u32[]{:S(2)}) collective-permute-start(bf16[1,48,1536]{2,1,0:T(8,128)(2,1)S(1)} %copy-done.7), channel_id=1, source_target_pairs={{0,256},{256,0},{1,257},{257,1},{2,258},{258,2},{3,259},{259,3},{4... | collective-permute-start | bytes 442376 | tf_op jit(solution)/shard_map/ppermute | solution.py:22
  64.8 7.8 %collective-permute-done = bf16[1,48,1536]{2,1,0:T(8,128)(2,1)S(1)} collective-permute-done((bf16[1,48,1536]{2,1,0:T(8,128)(2,1)S(1)}, bf16[1,48,1536]{2,1,0:T(8,128)(2,1)S(1)}, u32[]{:S(2)}, u32[]{:S(2)}) %collective-permute-start) | collective-permute-done | bytes 147488 | tf_op jit(solution)/shard_map/ppermute | solution.py:22
  72.6 3.5 %collective-permute-start.1 = (bf16[2,48,1536]{2,1,0:T(8,128)(2,1)S(1)}, bf16[2,48,1536]{2,1,0:T(8,128)(2,1)S(1)}, u32[]{:S(2)}, u32[]{:S(2)}) collective-permute-start(bf16[2,48,1536]{2,1,0:T(8,128)(2,1)S(1)} %constant_dynamic-update-slice_fusion.refs_0_), channel_id=1, source_target_pairs={{0,32},{32,64},{64,96},{96,128},{128,160},{160,192},{192,224},{224... | collective-permute-start | bytes 884744 | tf_op jit(solution)/shard_map/ppermute | solution.py:22
  76.1 2.5 %collective-permute-start.8 = (bf16[6,96,384]{2,1,0:T(8,128)(2,1)S(1)}, bf16[6,96,384]{2,1,0:T(8,128)(2,1)}, u32[]{:S(2)}, u32[]{:S(2)}) collective-permute-start(bf16[6,96,384]{2,1,0:T(8,128)(2,1)S(1)} %copy-done.1), channel_id=1, source_target_pairs={{0,1},{4,7},{1,2},{5,4},{2,3},{6,5},{3,0},{7,6},{8,9},{12,15},{9,1... | collective-permute-start | bytes 1327112 | tf_op jit(solution)/shard_map/ppermute | solution.py:28
  78.5 3.8 %collective-permute-start.5 = (bf16[2,48,1536]{2,1,0:T(8,128)(2,1)S(1)}, bf16[2,48,1536]{2,1,0:T(8,128)(2,1)}, u32[]{:S(2)}, u32[]{:S(2)}) collective-permute-start(bf16[2,48,1536]{2,1,0:T(8,128)(2,1)S(1)} %constant_dynamic-update-slice_fusion.refs_0_), channel_id=1, source_target_pairs={{0,224},{32,0},{64,32},{96,64},{128,96},{160,128},{192,160},{224,1... | collective-permute-start | bytes 884744 | tf_op jit(solution)/shard_map/ppermute | solution.py:22
  82.4 0.7 copy-done.2
  83.1 1.8 %collective-permute-done.1.refs_1_ = bf16[2,48,1536]{2,1,0:T(8,128)(2,1)S(1)} collective-permute-done((bf16[2,48,1536]{2,1,0:T(8,128)(2,1)S(1)}, bf16[2,48,1536]{2,1,0:T(8,128)(2,1)S(1)}, u32[]{:S(2)}, u32[]{:S(2)}) %collective-permute-start.1) | collective-permute-done | bytes 294944 | tf_op jit(solution)/shard_map/ppermute | solution.py:22
  84.9 1.9 %collective-permute-start.2 = (bf16[2,48,1536]{2,1,0:T(8,128)(2,1)S(1)}, bf16[2,48,1536]{2,1,0:T(8,128)(2,1)}, u32[]{:S(2)}, u32[]{:S(2)}) collective-permute-start(bf16[2,48,1536]{2,1,0:T(8,128)(2,1)S(1)} %collective-permute-done.1.refs_1_), channel_id=1, source_target_pairs={{0,32},{32,64},{64,96},{96,128},{128,160},{160,192},{192,224},{224... | collective-permute-start | bytes 884744 | tf_op jit(solution)/shard_map/ppermute | solution.py:22
  86.8 0.7 copy-done.4
  87.5 1.8 %collective-permute-done.5.refs_4_ = bf16[2,48,1536]{2,1,0:T(8,128)(2,1)} collective-permute-done((bf16[2,48,1536]{2,1,0:T(8,128)(2,1)S(1)}, bf16[2,48,1536]{2,1,0:T(8,128)(2,1)}, u32[]{:S(2)}, u32[]{:S(2)}) %collective-permute-start.5) | collective-permute-done | bytes 294944 | tf_op jit(solution)/shard_map/ppermute | solution.py:22
  89.3 5.3 %collective-permute-start.6 = (bf16[2,48,1536]{2,1,0:T(8,128)(2,1)}, bf16[2,48,1536]{2,1,0:T(8,128)(2,1)}, u32[]{:S(2)}, u32[]{:S(2)}) collective-permute-start(bf16[2,48,1536]{2,1,0:T(8,128)(2,1)} %collective-permute-done.5.refs_4_), channel_id=1, source_target_pairs={{0,224},{32,0},{64,32},{96,64},{128,96},{160,128},{192,160},{224,1... | collective-permute-start | bytes 884744 | tf_op jit(solution)/shard_map/ppermute | solution.py:22
  94.6 1.7 %collective-permute-done.2.refs_2_ = bf16[2,48,1536]{2,1,0:T(8,128)(2,1)} collective-permute-done((bf16[2,48,1536]{2,1,0:T(8,128)(2,1)S(1)}, bf16[2,48,1536]{2,1,0:T(8,128)(2,1)}, u32[]{:S(2)}, u32[]{:S(2)}) %collective-permute-start.2) | collective-permute-done | bytes 294944 | tf_op jit(solution)/shard_map/ppermute | solution.py:22
  96.3 1.9 %collective-permute-start.3 = (bf16[2,48,1536]{2,1,0:T(8,128)(2,1)}, bf16[2,48,1536]{2,1,0:T(8,128)(2,1)}, u32[]{:S(2)}, u32[]{:S(2)}) collective-permute-start(bf16[2,48,1536]{2,1,0:T(8,128)(2,1)} %collective-permute-done.2.refs_2_), channel_id=1, source_target_pairs={{0,32},{32,64},{64,96},{96,128},{128,160},{160,192},{192,224},{224... | collective-permute-start | bytes 884744 | tf_op jit(solution)/shard_map/ppermute | solution.py:22
  98.2 2.6 %collective-permute-start.10 = (bf16[3,96,384]{2,1,0:T(8,128)(2,1)S(1)}, bf16[3,96,384]{2,1,0:T(8,128)(2,1)S(1)}, u32[]{:S(2)}, u32[]{:S(2)}) collective-permute-start(bf16[3,96,384]{2,1,0:T(8,128)(2,1)S(1)} %constant_dynamic-slice_fusion.1), channel_id=1, source_target_pairs={{0,2},{1,3},{2,0},{3,1},{4,6},{5,7},{6,4},{7,5},{8,10},{9,11},{10,... | collective-permute-start | bytes 663560 | tf_op jit(solution)/shard_map/ppermute | solution.py:22
  100.9 1.9 %collective-permute-start.9 = (bf16[6,96,384]{2,1,0:T(8,128)(2,1)}, bf16[6,96,384]{2,1,0:T(8,128)(2,1)S(1)}, u32[]{:S(2)}, u32[]{:S(2)}) collective-permute-start(bf16[6,96,384]{2,1,0:T(8,128)(2,1)} %collective-permute-done.8.refs_6_.refs_4_), channel_id=1, source_target_pairs={{0,4},{4,0},{1,5},{5,1},{2,6},{6,2},{3,7},{7,3},{8,12},{12,8},{9,1... | collective-permute-start | bytes 1327112 | tf_op jit(solution)/shard_map/ppermute | solution.py:22
  102.8 5.1 %collective-permute-start.7 = (bf16[2,48,1536]{2,1,0:T(8,128)(2,1)}, bf16[2,48,1536]{2,1,0:T(8,128)(2,1)S(1)}, u32[]{:S(2)}, u32[]{:S(2)}) collective-permute-start(bf16[2,48,1536]{2,1,0:T(8,128)(2,1)} %collective-permute-done.6.refs_3_), channel_id=1, source_target_pairs={{0,224},{32,0},{64,32},{96,64},{128,96},{160,128},{192,160},{224,1... | collective-permute-start | bytes 884744 | tf_op jit(solution)/shard_map/ppermute | solution.py:22
  108.0 1.9 %collective-permute-start.4 = (bf16[2,48,1536]{2,1,0:T(8,128)(2,1)}, bf16[2,48,1536]{2,1,0:T(8,128)(2,1)S(1)}, u32[]{:S(2)}, u32[]{:S(2)}) collective-permute-start(bf16[2,48,1536]{2,1,0:T(8,128)(2,1)} %collective-permute-done.3.refs_0_), channel_id=1, source_target_pairs={{0,32},{32,64},{64,96},{96,128},{128,160},{160,192},{192,224},{224... | collective-permute-start | bytes 884744 | tf_op jit(solution)/shard_map/ppermute | solution.py:22
  109.9 2.1 %collective-permute-start.11 = (bf16[3,96,384]{2,1,0:T(8,128)(2,1)S(1)}, bf16[3,96,384]{2,1,0:T(8,128)(2,1)S(1)}, u32[]{:S(2)}, u32[]{:S(2)}) collective-permute-start(bf16[3,96,384]{2,1,0:T(8,128)(2,1)S(1)} %collective-permute-done.10.refs_8_.refs_6_), channel_id=1, source_target_pairs={{0,4},{4,0},{1,5},{5,1},{2,6},{6,2},{3,7},{7,3},{8,12},{12,8},{9,1... | collective-permute-start | bytes 663560 | tf_op jit(solution)/shard_map/ppermute | solution.py:22
  112.1 1.2 collective-permute-done.11.refs_9_.refs_7_
  113.3 1.0 copy-done.3
  114.3 1.0 copy-done.5
  115.2 3.1 %shard_map.46.refs_8_ = bf16[16,288,96]{2,1,0:T(8,128)(2,1)S(1)} custom-call(s32[4,8]{1,0:T(4,128)S(1)} %bitcast.4, bf16[2,48,1536]{2,1,0:T(8,128)(2,1)S(1)} %copy-done.3, bf16[2,48,1536]{2,1,0:T(8,128)(2,1)S(1)} %copy-done.5, bf16[2,48,1536]{2,1,0:T(8,128)(2,1)} %collective-permute-done.2.refs_2_, bf16[2,48,1536]{2,1,0:T(8,128)(2,1)} %collective-permute-done.6.refs_3_, ...), custom_call_target="tpu_custom_call" | custom-call | tf_op jit(solution)/shard_map/pallas_call | solution.py:85
  118.4 2.1 %collective-permute-done.4.refs_1_ = bf16[2,48,1536]{2,1,0:T(8,128)(2,1)S(1)} collective-permute-done((bf16[2,48,1536]{2,1,0:T(8,128)(2,1)}, bf16[2,48,1536]{2,1,0:T(8,128)(2,1)S(1)}, u32[]{:S(2)}, u32[]{:S(2)}) %collective-permute-start.4) | collective-permute-done | bytes 294944 | tf_op jit(solution)/shard_map/ppermute | solution.py:22
  120.4 2.4 %shard_map.47.half = bf16[16,288,96]{2,1,0:T(8,128)(2,1)S(1)} custom-call(s32[4,8]{1,0:T(4,128)S(1)} %bitcast.5, bf16[2,48,1536]{2,1,0:T(8,128)(2,1)} %collective-permute-done.3.refs_0_, bf16[2,48,1536]{2,1,0:T(8,128)(2,1)S(1)} %collective-permute-done.4.refs_1_, bf16[2,48,1536]{2,1,0:T(8,128)(2,1)S(1)} %collective-permute-done.7.refs_2_, ...), custom_call_target="tpu_custom_call" | custom-call | tf_op jit(solution)/shard_map/pallas_call | solution.py:85
  122.8 4.2 %total.1 = bf16[16,216,128]{2,1,0:T(8,128)(2,1)S(1)} custom-call(bf16[16,288,96]{2,1,0:T(8,128)(2,1)S(1)} %shard_map.47.half, bf16[4,4,2,96,384]{4,3,2,1,0:T(8,128)(2,1)S(1)} %all_to_all.16.mine, bf16[4,4,2,96,384]{4,3,2,1,0:T(8,128)(2,1)} %collective-permute-done.12.theirs), custom_call_target="tpu_custom_call" | custom-call | tf_op jit(solution)/shard_map/total/pallas_call | solution.py:157
  127.0 39.5 %all_to_all.17.parts = bf16[16,216,128]{2,1,0:T(8,128)(2,1)S(1)} all-to-all(bf16[16,216,128]{2,1,0:T(8,128)(2,1)S(1)} %total.1), channel_id=1, replica_groups=mesh['zh'=2,'y'=8,'zl'=4,'core'=2,'x'=4] {'y','zh'}, dimensions={0} | all-to-all | bytes 1769472 | tf_op jit(solution)/shard_map/all_to_all | solution.py:166
  166.6 0.8 sum.1
  (23 shorter events, 0.2 us)
Async XLA Ops:
  0.0 1.1 copy-start
  22.4 34.1 %copy-start.7 = (bf16[1,48,1536]{2,1,0:T(8,128)(2,1)S(1)}, bf16[1,48,1536]{2,1,0:T(8,128)(2,1)}, u32[]{:S(2)}) copy-start(bf16[1,48,1536]{2,1,0:T(8,128)(2,1)} %param.6) | copy-start | bytes 442372
  22.5 53.6 %copy-start.1 = (bf16[6,96,384]{2,1,0:T(8,128)(2,1)S(1)}, bf16[6,96,384]{2,1,0:T(8,128)(2,1)}, u32[]{:S(2)}) copy-start(bf16[6,96,384]{2,1,0:T(8,128)(2,1)} %refs_3_.1) | copy-start | bytes 1327108
  22.5 90.8 %copy-start.6 = (s32[8,4]{0,1:T(4,128)S(1)}, s32[8,4]{0,1:T(4,128)}, u32[]{:S(2)}) copy-start(s32[8,4]{0,1:T(4,128)} %param.7) | copy-start | bytes 388
  54.6 68.2 %collective-permute-start.12 = (bf16[4,4,2,96,384]{4,3,2,1,0:T(8,128)(2,1)S(1)}, bf16[4,4,2,96,384]{4,3,2,1,0:T(8,128)(2,1)}, u32[]{:S(2)}, u32[]{:S(2)}) collective-permute-start(bf16[4,4,2,96,384]{4,3,2,1,0:T(8,128)(2,1)S(1)} %all_to_all.16.mine), channel_id=1, source_target_pairs={{0,4},{4,0},{1,5},{5,1},{2,6},{6,2},{3,7},{7,3},{8,12},{12,8},{9,1... | collective-permute-start | bytes 7077896 | tf_op jit(solution)/shard_map/ppermute | solution.py:22
  56.5 16.0 %collective-permute-start = (bf16[1,48,1536]{2,1,0:T(8,128)(2,1)S(1)}, bf16[1,48,1536]{2,1,0:T(8,128)(2,1)S(1)}, u32[]{:S(2)}, u32[]{:S(2)}) collective-permute-start(bf16[1,48,1536]{2,1,0:T(8,128)(2,1)S(1)} %copy-done.7), channel_id=1, source_target_pairs={{0,256},{256,0},{1,257},{257,1},{2,258},{258,2},{3,259},{259,3},{4... | collective-permute-start | bytes 442376 | tf_op jit(solution)/shard_map/ppermute | solution.py:22
  72.6 12.3 %collective-permute-start.1 = (bf16[2,48,1536]{2,1,0:T(8,128)(2,1)S(1)}, bf16[2,48,1536]{2,1,0:T(8,128)(2,1)S(1)}, u32[]{:S(2)}, u32[]{:S(2)}) collective-permute-start(bf16[2,48,1536]{2,1,0:T(8,128)(2,1)S(1)} %constant_dynamic-update-slice_fusion.refs_0_), channel_id=1, source_target_pairs={{0,32},{32,64},{64,96},{96,128},{128,160},{160,192},{192,224},{224... | collective-permute-start | bytes 884744 | tf_op jit(solution)/shard_map/ppermute | solution.py:22
  76.1 24.8 %collective-permute-start.8 = (bf16[6,96,384]{2,1,0:T(8,128)(2,1)S(1)}, bf16[6,96,384]{2,1,0:T(8,128)(2,1)}, u32[]{:S(2)}, u32[]{:S(2)}) collective-permute-start(bf16[6,96,384]{2,1,0:T(8,128)(2,1)S(1)} %copy-done.1), channel_id=1, source_target_pairs={{0,1},{4,7},{1,2},{5,4},{2,3},{6,5},{3,0},{7,6},{8,9},{12,15},{9,1... | collective-permute-start | bytes 1327112 | tf_op jit(solution)/shard_map/ppermute | solution.py:28
  78.5 10.7 %collective-permute-start.5 = (bf16[2,48,1536]{2,1,0:T(8,128)(2,1)S(1)}, bf16[2,48,1536]{2,1,0:T(8,128)(2,1)}, u32[]{:S(2)}, u32[]{:S(2)}) collective-permute-start(bf16[2,48,1536]{2,1,0:T(8,128)(2,1)S(1)} %constant_dynamic-update-slice_fusion.refs_0_), channel_id=1, source_target_pairs={{0,224},{32,0},{64,32},{96,64},{128,96},{160,128},{192,160},{224,1... | collective-permute-start | bytes 884744 | tf_op jit(solution)/shard_map/ppermute | solution.py:22
  82.4 0.7 copy-start.2
  84.9 11.4 %collective-permute-start.2 = (bf16[2,48,1536]{2,1,0:T(8,128)(2,1)S(1)}, bf16[2,48,1536]{2,1,0:T(8,128)(2,1)}, u32[]{:S(2)}, u32[]{:S(2)}) collective-permute-start(bf16[2,48,1536]{2,1,0:T(8,128)(2,1)S(1)} %collective-permute-done.1.refs_1_), channel_id=1, source_target_pairs={{0,32},{32,64},{64,96},{96,128},{128,160},{160,192},{192,224},{224... | collective-permute-start | bytes 884744 | tf_op jit(solution)/shard_map/ppermute | solution.py:22
  86.8 0.7 copy-start.4
  89.3 13.5 %collective-permute-start.6 = (bf16[2,48,1536]{2,1,0:T(8,128)(2,1)}, bf16[2,48,1536]{2,1,0:T(8,128)(2,1)}, u32[]{:S(2)}, u32[]{:S(2)}) collective-permute-start(bf16[2,48,1536]{2,1,0:T(8,128)(2,1)} %collective-permute-done.5.refs_4_), channel_id=1, source_target_pairs={{0,224},{32,0},{64,32},{96,64},{128,96},{160,128},{192,160},{224,1... | collective-permute-start | bytes 884744 | tf_op jit(solution)/shard_map/ppermute | solution.py:22
  96.3 11.7 %collective-permute-start.3 = (bf16[2,48,1536]{2,1,0:T(8,128)(2,1)}, bf16[2,48,1536]{2,1,0:T(8,128)(2,1)}, u32[]{:S(2)}, u32[]{:S(2)}) collective-permute-start(bf16[2,48,1536]{2,1,0:T(8,128)(2,1)} %collective-permute-done.2.refs_2_), channel_id=1, source_target_pairs={{0,32},{32,64},{64,96},{96,128},{128,160},{160,192},{192,224},{224... | collective-permute-start | bytes 884744 | tf_op jit(solution)/shard_map/ppermute | solution.py:22
  98.2 11.7 %collective-permute-start.10 = (bf16[3,96,384]{2,1,0:T(8,128)(2,1)S(1)}, bf16[3,96,384]{2,1,0:T(8,128)(2,1)S(1)}, u32[]{:S(2)}, u32[]{:S(2)}) collective-permute-start(bf16[3,96,384]{2,1,0:T(8,128)(2,1)S(1)} %constant_dynamic-slice_fusion.1), channel_id=1, source_target_pairs={{0,2},{1,3},{2,0},{3,1},{4,6},{5,7},{6,4},{7,5},{8,10},{9,11},{10,... | collective-permute-start | bytes 663560 | tf_op jit(solution)/shard_map/ppermute | solution.py:22
  100.9 12.4 %collective-permute-start.9 = (bf16[6,96,384]{2,1,0:T(8,128)(2,1)}, bf16[6,96,384]{2,1,0:T(8,128)(2,1)S(1)}, u32[]{:S(2)}, u32[]{:S(2)}) collective-permute-start(bf16[6,96,384]{2,1,0:T(8,128)(2,1)} %collective-permute-done.8.refs_6_.refs_4_), channel_id=1, source_target_pairs={{0,4},{4,0},{1,5},{5,1},{2,6},{6,2},{3,7},{7,3},{8,12},{12,8},{9,1... | collective-permute-start | bytes 1327112 | tf_op jit(solution)/shard_map/ppermute | solution.py:22
  102.8 15.5 %collective-permute-start.7 = (bf16[2,48,1536]{2,1,0:T(8,128)(2,1)}, bf16[2,48,1536]{2,1,0:T(8,128)(2,1)S(1)}, u32[]{:S(2)}, u32[]{:S(2)}) collective-permute-start(bf16[2,48,1536]{2,1,0:T(8,128)(2,1)} %collective-permute-done.6.refs_3_), channel_id=1, source_target_pairs={{0,224},{32,0},{64,32},{96,64},{128,96},{160,128},{192,160},{224,1... | collective-permute-start | bytes 884744 | tf_op jit(solution)/shard_map/ppermute | solution.py:22
  108.0 12.4 %collective-permute-start.4 = (bf16[2,48,1536]{2,1,0:T(8,128)(2,1)}, bf16[2,48,1536]{2,1,0:T(8,128)(2,1)S(1)}, u32[]{:S(2)}, u32[]{:S(2)}) collective-permute-start(bf16[2,48,1536]{2,1,0:T(8,128)(2,1)} %collective-permute-done.3.refs_0_), channel_id=1, source_target_pairs={{0,32},{32,64},{64,96},{96,128},{128,160},{160,192},{192,224},{224... | collective-permute-start | bytes 884744 | tf_op jit(solution)/shard_map/ppermute | solution.py:22
  109.9 3.4 %collective-permute-start.11 = (bf16[3,96,384]{2,1,0:T(8,128)(2,1)S(1)}, bf16[3,96,384]{2,1,0:T(8,128)(2,1)S(1)}, u32[]{:S(2)}, u32[]{:S(2)}) collective-permute-start(bf16[3,96,384]{2,1,0:T(8,128)(2,1)S(1)} %collective-permute-done.10.refs_8_.refs_6_), channel_id=1, source_target_pairs={{0,4},{4,0},{1,5},{5,1},{2,6},{6,2},{3,7},{7,3},{8,12},{12,8},{9,1... | collective-permute-start | bytes 663560 | tf_op jit(solution)/shard_map/ppermute | solution.py:22
  113.3 1.0 copy-start.3
  114.3 1.0 copy-start.5
where the time goes:
time: 168 us; the launch traced here: 167 us
  blocking collectives  92.6 us (55%)
  starting transfers between devices  42.7 us (25%)
  waiting for transfers between devices  16.4 us (10%)
  Pallas kernels  10.6 us (6%)
  local copies, waits for them, and re-layouts  4.86 us (3%)
    all_to_all x2, blocking collectives, copies_from(): return lax.all_to_all(copies, axis, 0, 0, tiled=True)  53.1 us
    ppermute x12, starting transfers between devices, shifted(): return lax.ppermute(block, axis, [(i, (i + by) % n) for i in range(n)])  40.3 us
    all_to_all x1, blocking collectives, per_device(): total = lax.all_to_all(total, ('y', 'zh'), 0, 0, tiled=True)  39.5 us
    ppermute x12, waiting for transfers between devices, shifted(): return lax.ppermute(block, axis, [(i, (i + by) % n) for i in range(n)])  16.4 us
    pallas_call x2, Pallas kernels, half_of(): pl.pallas_call(functools.partial(half_kernel, steps), in_specs=[SMEM] + [...  5.52 us
    unnamed x17, local copies, waits for them, and re-layouts  4.43 us
    pallas_call x1, Pallas kernels, per_device(): pl.pallas_call(total_kernel, in_specs=[VMEM] * 3, out_specs=VMEM, out_sha...  4.2 us
  transfers between devices with their start and end apart: 13, of which 6 were waited for; matrix products, arithmetic and copies ran while one was open for 0% of the time, Pallas kernels for 3%

commit v1 on v0

--- a/solution.py
+++ b/solution.py
@@ -114,8 +114,7 @@
         for i in range(width // rows):
             block = sums[:, i * rows : (i + 1) * rows]
             tail = jnp.concatenate([block[keep:, 32 * s : 32 * s + 32] for s in range(rows // 32)], axis=0)
-            va = x * (width // rows) + i
-            out[va % 8 * 2 + va // 8] = jnp.concatenate([block[:keep], tail], axis=1).astype(BF16)
+            out[x * (width // rows) + i] = jnp.concatenate([block[:keep], tail], axis=1).astype(BF16)
 
 
 def sum_kernel(parts, out):
@@ -163,7 +162,7 @@
         compiler_params=PARAMS,
         name="total",
     )(half, bra, bra_other)
-    total = lax.all_to_all(total, ("y", "zh"), 0, 0, tiled=True)
+    total = lax.all_to_all(total, VA, 0, 0, tiled=True)
     out = pl.pallas_call(
         sum_kernel,
         in_specs=[VMEM],

time: 168 us -> 166 us (0.988)
  the two profiles are of different devices: /device:TPU:64 before, /device:TPU:72 now
where the time goes in v1:
time: 166 us
  blocking collectives  93.3 us (56%)
  starting transfers between devices  40.5 us (24%)
  waiting for transfers between devices  16.1 us (10%)
  Pallas kernels  10.6 us (6%)
  local copies, waits for them, and re-layouts  4.86 us (3%)
    all_to_all x2, blocking collectives, copies_from(): return lax.all_to_all(copies, axis, 0, 0, tiled=True)  53.1 us
    all_to_all x1, blocking collectives, per_device(): total = lax.all_to_all(total, VA, 0, 0, tiled=True)  40.2 us
    ppermute x12, starting transfers between devices, shifted(): return lax.ppermute(block, axis, [(i, (i + by) % n) for i in range(n)])  38 us
    ppermute x12, waiting for transfers between devices, shifted(): return lax.ppermute(block, axis, [(i, (i + by) % n) for i in range(n)])  16.1 us
    pallas_call x2, Pallas kernels, half_of(): pl.pallas_call(functools.partial(half_kernel, steps), in_specs=[SMEM] + [...  5.52 us
    unnamed x17, local copies, waits for them, and re-layouts  4.43 us
    pallas_call x1, Pallas kernels, per_device(): pl.pallas_call(total_kernel, in_specs=[VMEM] * 3, out_specs=VMEM, out_sha...  4.2 us
  transfers between devices with their start and end apart: 13, of which 6 were waited for; matrix products, arithmetic and copies ran while one was open for 0% of the time, Pallas kernels for 3%

profile of v1, /device:TPU:72, one launch (start us, length us, event | category | flops | bytes accessed | tf_op | source)
XLA Modules:
  0.0 165.6 jit_solution(5303358863512105330)
XLA Ops:
  0.0 1.1 copy-done
  1.1 21.0 %all_to_all.15 = bf16[4,2,96,384]{3,2,1,0:T(8,128)(2,1)S(1)} all-to-all(bf16[4,2,96,384]{3,2,1,0:T(8,128)(2,1)S(1)} %broadcast_in_dim.6), channel_id=1, replica_groups=mesh['zh'=2,'y'=8,'zl'=4,'core'=2,'x'=4] {'zl'}, dimensions={0} | all-to-all | bytes 1179648 | tf_op jit(solution)/shard_map/all_to_all | solution.py:33
  22.1 0.3 broadcast_in_dim.7
  22.5 32.1 %all_to_all.16.mine = bf16[4,4,2,96,384]{4,3,2,1,0:T(8,128)(2,1)S(1)} all-to-all(bf16[4,4,2,96,384]{4,3,2,1,0:T(8,128)(2,1)S(1)} %broadcast_in_dim.7), channel_id=1, replica_groups=mesh['zh'=2,'y'=8,'zl'=4,'core'=2,'x'=4] {'x'}, dimensions={0} | all-to-all | bytes 4718592 | tf_op jit(solution)/shard_map/all_to_all | solution.py:33
  54.6 1.9 %collective-permute-start.12 = (bf16[4,4,2,96,384]{4,3,2,1,0:T(8,128)(2,1)S(1)}, bf16[4,4,2,96,384]{4,3,2,1,0:T(8,128)(2,1)}, u32[]{:S(2)}, u32[]{:S(2)}) collective-permute-start(bf16[4,4,2,96,384]{4,3,2,1,0:T(8,128)(2,1)S(1)} %all_to_all.16.mine), channel_id=1, source_target_pairs={{0,4},{4,0},{1,5},{5,1},{2,6},{6,2},{3,7},{7,3},{8,12},{12,8},{9,1... | collective-permute-start | bytes 7077896 | tf_op jit(solution)/shard_map/ppermute | solution.py:22
  56.5 8.2 %collective-permute-start = (bf16[1,48,1536]{2,1,0:T(8,128)(2,1)S(1)}, bf16[1,48,1536]{2,1,0:T(8,128)(2,1)S(1)}, u32[]{:S(2)}, u32[]{:S(2)}) collective-permute-start(bf16[1,48,1536]{2,1,0:T(8,128)(2,1)S(1)} %copy-done.7), channel_id=1, source_target_pairs={{0,256},{256,0},{1,257},{257,1},{2,258},{258,2},{3,259},{259,3},{4... | collective-permute-start | bytes 442376 | tf_op jit(solution)/shard_map/ppermute | solution.py:22
  64.8 7.8 %collective-permute-done = bf16[1,48,1536]{2,1,0:T(8,128)(2,1)S(1)} collective-permute-done((bf16[1,48,1536]{2,1,0:T(8,128)(2,1)S(1)}, bf16[1,48,1536]{2,1,0:T(8,128)(2,1)S(1)}, u32[]{:S(2)}, u32[]{:S(2)}) %collective-permute-start) | collective-permute-done | bytes 147488 | tf_op jit(solution)/shard_map/ppermute | solution.py:22
  72.6 3.5 %collective-permute-start.1 = (bf16[2,48,1536]{2,1,0:T(8,128)(2,1)S(1)}, bf16[2,48,1536]{2,1,0:T(8,128)(2,1)S(1)}, u32[]{:S(2)}, u32[]{:S(2)}) collective-permute-start(bf16[2,48,1536]{2,1,0:T(8,128)(2,1)S(1)} %constant_dynamic-update-slice_fusion.refs_0_), channel_id=1, source_target_pairs={{0,32},{32,64},{64,96},{96,128},{128,160},{160,192},{192,224},{224... | collective-permute-start | bytes 884744 | tf_op jit(solution)/shard_map/ppermute | solution.py:22
  76.1 2.5 %collective-permute-start.8 = (bf16[6,96,384]{2,1,0:T(8,128)(2,1)S(1)}, bf16[6,96,384]{2,1,0:T(8,128)(2,1)}, u32[]{:S(2)}, u32[]{:S(2)}) collective-permute-start(bf16[6,96,384]{2,1,0:T(8,128)(2,1)S(1)} %copy-done.1), channel_id=1, source_target_pairs={{0,1},{4,7},{1,2},{5,4},{2,3},{6,5},{3,0},{7,6},{8,9},{12,15},{9,1... | collective-permute-start | bytes 1327112 | tf_op jit(solution)/shard_map/ppermute | solution.py:28
  78.5 2.4 %collective-permute-start.5 = (bf16[2,48,1536]{2,1,0:T(8,128)(2,1)S(1)}, bf16[2,48,1536]{2,1,0:T(8,128)(2,1)}, u32[]{:S(2)}, u32[]{:S(2)}) collective-permute-start(bf16[2,48,1536]{2,1,0:T(8,128)(2,1)S(1)} %constant_dynamic-update-slice_fusion.refs_0_), channel_id=1, source_target_pairs={{0,224},{32,0},{64,32},{96,64},{128,96},{160,128},{192,160},{224,1... | collective-permute-start | bytes 884744 | tf_op jit(solution)/shard_map/ppermute | solution.py:22
  80.9 0.7 copy-done.2
  81.6 1.5 collective-permute-done.1.refs_1_
  83.1 3.5 %collective-permute-start.2 = (bf16[2,48,1536]{2,1,0:T(8,128)(2,1)S(1)}, bf16[2,48,1536]{2,1,0:T(8,128)(2,1)}, u32[]{:S(2)}, u32[]{:S(2)}) collective-permute-start(bf16[2,48,1536]{2,1,0:T(8,128)(2,1)S(1)} %collective-permute-done.1.refs_1_), channel_id=1, source_target_pairs={{0,32},{32,64},{64,96},{96,128},{128,160},{160,192},{192,224},{224... | collective-permute-start | bytes 884744 | tf_op jit(solution)/shard_map/ppermute | solution.py:22
  86.6 0.7 copy-done.4
  87.3 1.9 %collective-permute-done.5.refs_4_ = bf16[2,48,1536]{2,1,0:T(8,128)(2,1)} collective-permute-done((bf16[2,48,1536]{2,1,0:T(8,128)(2,1)S(1)}, bf16[2,48,1536]{2,1,0:T(8,128)(2,1)}, u32[]{:S(2)}, u32[]{:S(2)}) %collective-permute-start.5) | collective-permute-done | bytes 294944 | tf_op jit(solution)/shard_map/ppermute | solution.py:22
  89.3 2.3 %collective-permute-start.6 = (bf16[2,48,1536]{2,1,0:T(8,128)(2,1)}, bf16[2,48,1536]{2,1,0:T(8,128)(2,1)}, u32[]{:S(2)}, u32[]{:S(2)}) collective-permute-start(bf16[2,48,1536]{2,1,0:T(8,128)(2,1)} %collective-permute-done.5.refs_4_), channel_id=1, source_target_pairs={{0,224},{32,0},{64,32},{96,64},{128,96},{160,128},{192,160},{224,1... | collective-permute-start | bytes 884744 | tf_op jit(solution)/shard_map/ppermute | solution.py:22
  91.6 2.2 %collective-permute-done.2.refs_2_ = bf16[2,48,1536]{2,1,0:T(8,128)(2,1)} collective-permute-done((bf16[2,48,1536]{2,1,0:T(8,128)(2,1)S(1)}, bf16[2,48,1536]{2,1,0:T(8,128)(2,1)}, u32[]{:S(2)}, u32[]{:S(2)}) %collective-permute-start.2) | collective-permute-done | bytes 294944 | tf_op jit(solution)/shard_map/ppermute | solution.py:22
  93.8 2.6 %collective-permute-start.3 = (bf16[2,48,1536]{2,1,0:T(8,128)(2,1)}, bf16[2,48,1536]{2,1,0:T(8,128)(2,1)}, u32[]{:S(2)}, u32[]{:S(2)}) collective-permute-start(bf16[2,48,1536]{2,1,0:T(8,128)(2,1)} %collective-permute-done.2.refs_2_), channel_id=1, source_target_pairs={{0,32},{32,64},{64,96},{96,128},{128,160},{160,192},{192,224},{224... | collective-permute-start | bytes 884744 | tf_op jit(solution)/shard_map/ppermute | solution.py:22
  96.5 2.8 %collective-permute-start.10 = (bf16[3,96,384]{2,1,0:T(8,128)(2,1)S(1)}, bf16[3,96,384]{2,1,0:T(8,128)(2,1)S(1)}, u32[]{:S(2)}, u32[]{:S(2)}) collective-permute-start(bf16[3,96,384]{2,1,0:T(8,128)(2,1)S(1)} %constant_dynamic-slice_fusion.1), channel_id=1, source_target_pairs={{0,2},{1,3},{2,0},{3,1},{4,6},{5,7},{6,4},{7,5},{8,10},{9,11},{10,... | collective-permute-start | bytes 663560 | tf_op jit(solution)/shard_map/ppermute | solution.py:22
  99.3 1.9 %collective-permute-start.9 = (bf16[6,96,384]{2,1,0:T(8,128)(2,1)}, bf16[6,96,384]{2,1,0:T(8,128)(2,1)S(1)}, u32[]{:S(2)}, u32[]{:S(2)}) collective-permute-start(bf16[6,96,384]{2,1,0:T(8,128)(2,1)} %collective-permute-done.8.refs_6_.refs_4_), channel_id=1, source_target_pairs={{0,4},{4,0},{1,5},{5,1},{2,6},{6,2},{3,7},{7,3},{8,12},{12,8},{9,1... | collective-permute-start | bytes 1327112 | tf_op jit(solution)/shard_map/ppermute | solution.py:22
  101.3 3.9 %collective-permute-start.7 = (bf16[2,48,1536]{2,1,0:T(8,128)(2,1)}, bf16[2,48,1536]{2,1,0:T(8,128)(2,1)S(1)}, u32[]{:S(2)}, u32[]{:S(2)}) collective-permute-start(bf16[2,48,1536]{2,1,0:T(8,128)(2,1)} %collective-permute-done.6.refs_3_), channel_id=1, source_target_pairs={{0,224},{32,0},{64,32},{96,64},{128,96},{160,128},{192,160},{224,1... | collective-permute-start | bytes 884744 | tf_op jit(solution)/shard_map/ppermute | solution.py:22
  105.2 2.8 %collective-permute-start.4 = (bf16[2,48,1536]{2,1,0:T(8,128)(2,1)}, bf16[2,48,1536]{2,1,0:T(8,128)(2,1)S(1)}, u32[]{:S(2)}, u32[]{:S(2)}) collective-permute-start(bf16[2,48,1536]{2,1,0:T(8,128)(2,1)} %collective-permute-done.3.refs_0_), channel_id=1, source_target_pairs={{0,32},{32,64},{64,96},{96,128},{128,160},{160,192},{192,224},{224... | collective-permute-start | bytes 884744 | tf_op jit(solution)/shard_map/ppermute | solution.py:22
  108.0 2.1 %collective-permute-start.11 = (bf16[3,96,384]{2,1,0:T(8,128)(2,1)S(1)}, bf16[3,96,384]{2,1,0:T(8,128)(2,1)S(1)}, u32[]{:S(2)}, u32[]{:S(2)}) collective-permute-start(bf16[3,96,384]{2,1,0:T(8,128)(2,1)S(1)} %collective-permute-done.10.refs_8_.refs_6_), channel_id=1, source_target_pairs={{0,4},{4,0},{1,5},{5,1},{2,6},{6,2},{3,7},{7,3},{8,12},{12,8},{9,1... | collective-permute-start | bytes 663560 | tf_op jit(solution)/shard_map/ppermute | solution.py:22
  110.2 1.2 collective-permute-done.11.refs_9_.refs_7_
  111.4 1.0 copy-done.3
  112.4 1.0 copy-done.5
  113.3 3.1 %shard_map.46.refs_8_ = bf16[16,288,96]{2,1,0:T(8,128)(2,1)S(1)} custom-call(s32[4,8]{1,0:T(4,128)S(1)} %bitcast.4, bf16[2,48,1536]{2,1,0:T(8,128)(2,1)S(1)} %copy-done.3, bf16[2,48,1536]{2,1,0:T(8,128)(2,1)S(1)} %copy-done.5, bf16[2,48,1536]{2,1,0:T(8,128)(2,1)} %collective-permute-done.2.refs_2_, bf16[2,48,1536]{2,1,0:T(8,128)(2,1)} %collective-permute-done.6.refs_3_, ...), custom_call_target="tpu_custom_call" | custom-call | tf_op jit(solution)/shard_map/pallas_call | solution.py:85
  116.5 1.5 collective-permute-done.4.refs_1_
  117.9 2.4 %shard_map.47.half = bf16[16,288,96]{2,1,0:T(8,128)(2,1)S(1)} custom-call(s32[4,8]{1,0:T(4,128)S(1)} %bitcast.5, bf16[2,48,1536]{2,1,0:T(8,128)(2,1)} %collective-permute-done.3.refs_0_, bf16[2,48,1536]{2,1,0:T(8,128)(2,1)S(1)} %collective-permute-done.4.refs_1_, bf16[2,48,1536]{2,1,0:T(8,128)(2,1)S(1)} %collective-permute-done.7.refs_2_, ...), custom_call_target="tpu_custom_call" | custom-call | tf_op jit(solution)/shard_map/pallas_call | solution.py:85
  120.4 4.2 %total.1 = bf16[16,216,128]{2,1,0:T(8,128)(2,1)S(1)} custom-call(bf16[16,288,96]{2,1,0:T(8,128)(2,1)S(1)} %shard_map.47.half, bf16[4,4,2,96,384]{4,3,2,1,0:T(8,128)(2,1)S(1)} %all_to_all.16.mine, bf16[4,4,2,96,384]{4,3,2,1,0:T(8,128)(2,1)} %collective-permute-done.12.theirs), custom_call_target="tpu_custom_call" | custom-call | tf_op jit(solution)/shard_map/total/pallas_call | solution.py:156
  124.6 40.2 %all_to_all.17.parts = bf16[16,216,128]{2,1,0:T(8,128)(2,1)S(1)} all-to-all(bf16[16,216,128]{2,1,0:T(8,128)(2,1)S(1)} %total.1), channel_id=1, replica_groups=mesh['zh'=2,'y'=8,'zl'=4,'core'=2,'x'=4] {'zh','y'}, dimensions={0} | all-to-all | bytes 1769472 | tf_op jit(solution)/shard_map/all_to_all | solution.py:165
  164.8 0.8 sum.1
  (23 shorter events, 0.2 us)
Async XLA Ops:
  0.0 1.1 copy-start
  22.4 34.1 %copy-start.7 = (bf16[1,48,1536]{2,1,0:T(8,128)(2,1)S(1)}, bf16[1,48,1536]{2,1,0:T(8,128)(2,1)}, u32[]{:S(2)}) copy-start(bf16[1,48,1536]{2,1,0:T(8,128)(2,1)} %param.6) | copy-start | bytes 442372
  22.5 53.6 %copy-start.1 = (bf16[6,96,384]{2,1,0:T(8,128)(2,1)S(1)}, bf16[6,96,384]{2,1,0:T(8,128)(2,1)}, u32[]{:S(2)}) copy-start(bf16[6,96,384]{2,1,0:T(8,128)(2,1)} %refs_3_.1) | copy-start | bytes 1327108
  22.5 88.9 %copy-start.6 = (s32[8,4]{0,1:T(4,128)S(1)}, s32[8,4]{0,1:T(4,128)}, u32[]{:S(2)}) copy-start(s32[8,4]{0,1:T(4,128)} %param.7) | copy-start | bytes 388
  54.6 65.8 %collective-permute-start.12 = (bf16[4,4,2,96,384]{4,3,2,1,0:T(8,128)(2,1)S(1)}, bf16[4,4,2,96,384]{4,3,2,1,0:T(8,128)(2,1)}, u32[]{:S(2)}, u32[]{:S(2)}) collective-permute-start(bf16[4,4,2,96,384]{4,3,2,1,0:T(8,128)(2,1)S(1)} %all_to_all.16.mine), channel_id=1, source_target_pairs={{0,4},{4,0},{1,5},{5,1},{2,6},{6,2},{3,7},{7,3},{8,12},{12,8},{9,1... | collective-permute-start | bytes 7077896 | tf_op jit(solution)/shard_map/ppermute | solution.py:22
  56.5 16.0 %collective-permute-start = (bf16[1,48,1536]{2,1,0:T(8,128)(2,1)S(1)}, bf16[1,48,1536]{2,1,0:T(8,128)(2,1)S(1)}, u32[]{:S(2)}, u32[]{:S(2)}) collective-permute-start(bf16[1,48,1536]{2,1,0:T(8,128)(2,1)S(1)} %copy-done.7), channel_id=1, source_target_pairs={{0,256},{256,0},{1,257},{257,1},{2,258},{258,2},{3,259},{259,3},{4... | collective-permute-start | bytes 442376 | tf_op jit(solution)/shard_map/ppermute | solution.py:22
  72.6 10.6 %collective-permute-start.1 = (bf16[2,48,1536]{2,1,0:T(8,128)(2,1)S(1)}, bf16[2,48,1536]{2,1,0:T(8,128)(2,1)S(1)}, u32[]{:S(2)}, u32[]{:S(2)}) collective-permute-start(bf16[2,48,1536]{2,1,0:T(8,128)(2,1)S(1)} %constant_dynamic-update-slice_fusion.refs_0_), channel_id=1, source_target_pairs={{0,32},{32,64},{64,96},{96,128},{128,160},{160,192},{192,224},{224... | collective-permute-start | bytes 884744 | tf_op jit(solution)/shard_map/ppermute | solution.py:22
  76.1 23.3 %collective-permute-start.8 = (bf16[6,96,384]{2,1,0:T(8,128)(2,1)S(1)}, bf16[6,96,384]{2,1,0:T(8,128)(2,1)}, u32[]{:S(2)}, u32[]{:S(2)}) collective-permute-start(bf16[6,96,384]{2,1,0:T(8,128)(2,1)S(1)} %copy-done.1), channel_id=1, source_target_pairs={{0,1},{4,7},{1,2},{5,4},{2,3},{6,5},{3,0},{7,6},{8,9},{12,15},{9,1... | collective-permute-start | bytes 1327112 | tf_op jit(solution)/shard_map/ppermute | solution.py:28
  78.5 10.7 %collective-permute-start.5 = (bf16[2,48,1536]{2,1,0:T(8,128)(2,1)S(1)}, bf16[2,48,1536]{2,1,0:T(8,128)(2,1)}, u32[]{:S(2)}, u32[]{:S(2)}) collective-permute-start(bf16[2,48,1536]{2,1,0:T(8,128)(2,1)S(1)} %constant_dynamic-update-slice_fusion.refs_0_), channel_id=1, source_target_pairs={{0,224},{32,0},{64,32},{96,64},{128,96},{160,128},{192,160},{224,1... | collective-permute-start | bytes 884744 | tf_op jit(solution)/shard_map/ppermute | solution.py:22
  80.9 0.7 copy-start.2
  83.1 10.7 %collective-permute-start.2 = (bf16[2,48,1536]{2,1,0:T(8,128)(2,1)S(1)}, bf16[2,48,1536]{2,1,0:T(8,128)(2,1)}, u32[]{:S(2)}, u32[]{:S(2)}) collective-permute-start(bf16[2,48,1536]{2,1,0:T(8,128)(2,1)S(1)} %collective-permute-done.1.refs_1_), channel_id=1, source_target_pairs={{0,32},{32,64},{64,96},{96,128},{128,160},{160,192},{192,224},{224... | collective-permute-start | bytes 884744 | tf_op jit(solution)/shard_map/ppermute | solution.py:22
  86.6 0.7 copy-start.4
  89.3 12.0 %collective-permute-start.6 = (bf16[2,48,1536]{2,1,0:T(8,128)(2,1)}, bf16[2,48,1536]{2,1,0:T(8,128)(2,1)}, u32[]{:S(2)}, u32[]{:S(2)}) collective-permute-start(bf16[2,48,1536]{2,1,0:T(8,128)(2,1)} %collective-permute-done.5.refs_4_), channel_id=1, source_target_pairs={{0,224},{32,0},{64,32},{96,64},{128,96},{160,128},{192,160},{224,1... | collective-permute-start | bytes 884744 | tf_op jit(solution)/shard_map/ppermute | solution.py:22
  93.8 11.4 %collective-permute-start.3 = (bf16[2,48,1536]{2,1,0:T(8,128)(2,1)}, bf16[2,48,1536]{2,1,0:T(8,128)(2,1)}, u32[]{:S(2)}, u32[]{:S(2)}) collective-permute-start(bf16[2,48,1536]{2,1,0:T(8,128)(2,1)} %collective-permute-done.2.refs_2_), channel_id=1, source_target_pairs={{0,32},{32,64},{64,96},{96,128},{128,160},{160,192},{192,224},{224... | collective-permute-start | bytes 884744 | tf_op jit(solution)/shard_map/ppermute | solution.py:22
  96.5 11.5 %collective-permute-start.10 = (bf16[3,96,384]{2,1,0:T(8,128)(2,1)S(1)}, bf16[3,96,384]{2,1,0:T(8,128)(2,1)S(1)}, u32[]{:S(2)}, u32[]{:S(2)}) collective-permute-start(bf16[3,96,384]{2,1,0:T(8,128)(2,1)S(1)} %constant_dynamic-slice_fusion.1), channel_id=1, source_target_pairs={{0,2},{1,3},{2,0},{3,1},{4,6},{5,7},{6,4},{7,5},{8,10},{9,11},{10,... | collective-permute-start | bytes 663560 | tf_op jit(solution)/shard_map/ppermute | solution.py:22
  99.3 12.1 %collective-permute-start.9 = (bf16[6,96,384]{2,1,0:T(8,128)(2,1)}, bf16[6,96,384]{2,1,0:T(8,128)(2,1)S(1)}, u32[]{:S(2)}, u32[]{:S(2)}) collective-permute-start(bf16[6,96,384]{2,1,0:T(8,128)(2,1)} %collective-permute-done.8.refs_6_.refs_4_), channel_id=1, source_target_pairs={{0,4},{4,0},{1,5},{5,1},{2,6},{6,2},{3,7},{7,3},{8,12},{12,8},{9,1... | collective-permute-start | bytes 1327112 | tf_op jit(solution)/shard_map/ppermute | solution.py:22
  101.3 15.2 %collective-permute-start.7 = (bf16[2,48,1536]{2,1,0:T(8,128)(2,1)}, bf16[2,48,1536]{2,1,0:T(8,128)(2,1)S(1)}, u32[]{:S(2)}, u32[]{:S(2)}) collective-permute-start(bf16[2,48,1536]{2,1,0:T(8,128)(2,1)} %collective-permute-done.6.refs_3_), channel_id=1, source_target_pairs={{0,224},{32,0},{64,32},{96,64},{128,96},{160,128},{192,160},{224,1... | collective-permute-start | bytes 884744 | tf_op jit(solution)/shard_map/ppermute | solution.py:22
  105.2 12.7 %collective-permute-start.4 = (bf16[2,48,1536]{2,1,0:T(8,128)(2,1)}, bf16[2,48,1536]{2,1,0:T(8,128)(2,1)S(1)}, u32[]{:S(2)}, u32[]{:S(2)}) collective-permute-start(bf16[2,48,1536]{2,1,0:T(8,128)(2,1)} %collective-permute-done.3.refs_0_), channel_id=1, source_target_pairs={{0,32},{32,64},{64,96},{96,128},{128,160},{160,192},{192,224},{224... | collective-permute-start | bytes 884744 | tf_op jit(solution)/shard_map/ppermute | solution.py:22
  108.0 3.4 %collective-permute-start.11 = (bf16[3,96,384]{2,1,0:T(8,128)(2,1)S(1)}, bf16[3,96,384]{2,1,0:T(8,128)(2,1)S(1)}, u32[]{:S(2)}, u32[]{:S(2)}) collective-permute-start(bf16[3,96,384]{2,1,0:T(8,128)(2,1)S(1)} %collective-permute-done.10.refs_8_.refs_6_), channel_id=1, source_target_pairs={{0,4},{4,0},{1,5},{5,1},{2,6},{6,2},{3,7},{7,3},{8,12},{12,8},{9,1... | collective-permute-start | bytes 663560 | tf_op jit(solution)/shard_map/ppermute | solution.py:22
  111.4 1.0 copy-start.3
  112.4 1.0 copy-start.5

commit v2 on v1

--- a/solution.py
+++ b/solution.py
@@ -39,17 +39,18 @@
 
 def half_kernel(steps, lists, *refs):
     kets, refs = refs[: len(steps)], refs[len(steps) :]
-    own, near, near_other, far, far_other = refs[:5]
+    own, near, near_other, far = refs[:4]
     half = refs[-1]
     zh, y, _, core, x = [position(name) for name in AXES]
-    n_own, rows, width = far.shape
+    pairs, rows, width = own.shape
+    n_own = pairs // 2
     cols = kets[0].shape[1]
     step = 1 - 2 * core
     firsts = [n_own * core, n_own * (1 - core)]
     chunks = [(x, [own[pl.ds(f, n_own)] for f in firsts])]
     chunks.append((x - step, [near[pl.ds(f, n_own)] for f in firsts]))
     chunks.append((x + step, [near_other[pl.ds(f, n_own)] for f in firsts]))
-    chunks.append((x + 2, [far[...], far_other[...]]))
+    chunks.append((x + 2, [far[pl.ds(f, n_own)] for f in firsts]))
     out = None
     for place, taus in chunks:
         at = pl.multiple_of(((place + 4) % 4) * width, 128)
@@ -57,9 +58,9 @@
         rhs = jnp.concatenate(taus, axis=0).reshape(2 * n_own * rows, width)
         term = lax.dot_general(lhs, rhs, (((1,), (1,)), ((), ())), preferred_element_type=F32)
         out = term if out is None else out + term
-    if len(refs) > 6:
+    if len(refs) > 5:
         for d in set(range(8)) - set(steps):
-            half[2 * d : 2 * d + 2] = refs[5][2 * d : 2 * d + 2]
+            half[2 * d : 2 * d + 2] = refs[4][2 * d : 2 * d + 2]
     for n, d in enumerate(steps):
         for h in range(2):
             high = zh if h == 0 else 1 - zh
@@ -132,7 +133,6 @@
     pairs, rows, _ = amplitudes.shape
     cols = ket_factor.shape[1]
     n_a = bra_factor.shape[2]
-    core = lax.axis_index("core")
     n_own = n_a // lax.axis_size("x")
 
     ket = jnp.concatenate([ket_factor, shifted(ket_factor, "zh", 1)], axis=0)
@@ -145,9 +145,8 @@
     own = lax.dynamic_slice_in_dim(bra_factor, n_own * lax.axis_index("x"), n_own, 2)
     bra = copies_from(copies_from(own, "zl"), "x")
     near = both_ways(amplitudes)
-    far = lax.dynamic_slice_in_dim(amplitudes, core * (pairs // 2), pairs // 2, 0)
-    far = shifted(far, "x", 2)
-    taus = [amplitudes, near, shifted(near, "core", 1), far, shifted(far, "core", 1)]
+    far = both_ways(near)
+    taus = [amplitudes, near, shifted(near, "core", 1), far]
     bra_other = shifted(bra, "core", 1)
 
     half = half_of((0, 1, 2, 6, 7), pair_list.T, kets, taus, None)

time: 166 us -> 163 us (0.982)
  waiting for transfers between devices: 16.1 us -> 21.8 us
  local copies, waits for them, and re-layouts: 4.86 us -> 1.5 us
  Pallas kernels: 10.6 us -> 7.64 us
  starting transfers between devices: 40.5 us -> 38.3 us
    ppermute x12 -> x10, waiting for transfers between devices: 16.1 us -> 21.8 us  [shifted(): return lax.ppermute(block, axis, [(i, (i + by) % n) for i in range(n)])]
    ppermute x12 -> x10, starting transfers between devices: 38 us -> 33.4 us  [shifted(): return lax.ppermute(block, axis, [(i, (i + by) % n) for i in range(n)])]
    unnamed x17 -> x9, local copies, waits for them, and re-layouts: 4.43 us -> 1.09 us
    ppermute x1 -> x2, starting transfers between devices: 2.47 us -> 4.95 us  [both_ways(): return lax.ppermute(block, ('core', 'x'), route)]
    pallas_call x1, Pallas kernels: 4.2 us -> 2.54 us  [per_device(): pl.pallas_call(total_kernel, in_specs=[VMEM] * 3, out_specs=VMEM, out_sha...]
  transfers between devices with their start and end apart: 13 -> 12, of which waited for: 6 -> 6; matrix products, arithmetic and copies ran while one was open for 0% -> 0% of each run, Pallas kernels for 3% -> 3%
where the time goes in v2:
time: 163 us
  blocking collectives  93.3 us (57%)
  starting transfers between devices  38.3 us (23%)
  waiting for transfers between devices  21.8 us (13%)
  Pallas kernels  7.64 us (5%)
    all_to_all x2, blocking collectives, copies_from(): return lax.all_to_all(copies, axis, 0, 0, tiled=True)  53.1 us
    all_to_all x1, blocking collectives, per_device(): total = lax.all_to_all(total, VA, 0, 0, tiled=True)  40.2 us
    ppermute x10, starting transfers between devices, shifted(): return lax.ppermute(block, axis, [(i, (i + by) % n) for i in range(n)])  33.4 us
    ppermute x10, waiting for transfers between devices, shifted(): return lax.ppermute(block, axis, [(i, (i + by) % n) for i in range(n)])  21.8 us
    ppermute x2, starting transfers between devices, both_ways(): return lax.ppermute(block, ('core', 'x'), route)  4.95 us
    pallas_call x2, Pallas kernels, half_of(): pl.pallas_call(functools.partial(half_kernel, steps), in_specs=[SMEM] + [...  4.26 us
  transfers between devices with their start and end apart: 12, of which 6 were waited for; matrix products, arithmetic and copies ran while one was open for 0% of the time, Pallas kernels for 3%

profile of v2, /device:TPU:72, one launch (start us, length us, event | category | flops | bytes accessed | tf_op | source)
XLA Modules:
  0.0 162.8 jit_solution(12576316637312980336)
XLA Ops:
  0.0 1.1 copy-done
  1.1 0.1 broadcast_in_dim.6
  1.1 21.0 %all_to_all.15 = bf16[4,2,96,384]{3,2,1,0:T(8,128)(2,1)S(1)} all-to-all(bf16[4,2,96,384]{3,2,1,0:T(8,128)(2,1)S(1)} %broadcast_in_dim.6), channel_id=1, replica_groups=mesh['zh'=2,'y'=8,'zl'=4,'core'=2,'x'=4] {'zl'}, dimensions={0} | all-to-all | bytes 1179648 | tf_op jit(solution)/shard_map/all_to_all | solution.py:33
  22.1 0.3 broadcast_in_dim.7
  22.4 0.0 copy-start.3
  22.5 0.0 copy-start.1
  22.5 0.0 copy-start.2
  22.5 32.1 %all_to_all.16.mine = bf16[4,4,2,96,384]{4,3,2,1,0:T(8,128)(2,1)S(1)} all-to-all(bf16[4,4,2,96,384]{4,3,2,1,0:T(8,128)(2,1)S(1)} %broadcast_in_dim.7), channel_id=1, replica_groups=mesh['zh'=2,'y'=8,'zl'=4,'core'=2,'x'=4] {'x'}, dimensions={0} | all-to-all | bytes 4718592 | tf_op jit(solution)/shard_map/all_to_all | solution.py:33
  54.6 1.9 %collective-permute-start.11 = (bf16[4,4,2,96,384]{4,3,2,1,0:T(8,128)(2,1)S(1)}, bf16[4,4,2,96,384]{4,3,2,1,0:T(8,128)(2,1)S(1)}, u32[]{:S(2)}, u32[]{:S(2)}) collective-permute-start(bf16[4,4,2,96,384]{4,3,2,1,0:T(8,128)(2,1)S(1)} %all_to_all.16.mine), channel_id=1, source_target_pairs={{0,4},{4,0},{1,5},{5,1},{2,6},{6,2},{3,7},{7,3},{8,12},{12,8},{9,1... | collective-permute-start | bytes 7077896 | tf_op jit(solution)/shard_map/ppermute | solution.py:22
  56.5 8.2 %collective-permute-start = (bf16[1,48,1536]{2,1,0:T(8,128)(2,1)S(1)}, bf16[1,48,1536]{2,1,0:T(8,128)(2,1)S(1)}, u32[]{:S(2)}, u32[]{:S(2)}) collective-permute-start(bf16[1,48,1536]{2,1,0:T(8,128)(2,1)S(1)} %copy-done.3), channel_id=1, source_target_pairs={{0,256},{256,0},{1,257},{257,1},{2,258},{258,2},{3,259},{259,3},{4... | collective-permute-start | bytes 442376 | tf_op jit(solution)/shard_map/ppermute | solution.py:22
  64.8 7.8 %collective-permute-done = bf16[1,48,1536]{2,1,0:T(8,128)(2,1)S(1)} collective-permute-done((bf16[1,48,1536]{2,1,0:T(8,128)(2,1)S(1)}, bf16[1,48,1536]{2,1,0:T(8,128)(2,1)S(1)}, u32[]{:S(2)}, u32[]{:S(2)}) %collective-permute-start) | collective-permute-done | bytes 147488 | tf_op jit(solution)/shard_map/ppermute | solution.py:22
  72.6 3.5 %collective-permute-start.1 = (bf16[2,48,1536]{2,1,0:T(8,128)(2,1)S(1)}, bf16[2,48,1536]{2,1,0:T(8,128)(2,1)S(1)}, u32[]{:S(2)}, u32[]{:S(2)}) collective-permute-start(bf16[2,48,1536]{2,1,0:T(8,128)(2,1)S(1)} %constant_dynamic-update-slice_fusion.refs_0_), channel_id=1, source_target_pairs={{0,32},{32,64},{64,96},{96,128},{128,160},{160,192},{192,224},{224... | collective-permute-start | bytes 884744 | tf_op jit(solution)/shard_map/ppermute | solution.py:22
  76.1 2.5 %collective-permute-start.8 = (bf16[6,96,384]{2,1,0:T(8,128)(2,1)S(1)}, bf16[6,96,384]{2,1,0:T(8,128)(2,1)S(1)}, u32[]{:S(2)}, u32[]{:S(2)}) collective-permute-start(bf16[6,96,384]{2,1,0:T(8,128)(2,1)S(1)} %copy-done.1), channel_id=1, source_target_pairs={{0,1},{4,7},{1,2},{5,4},{2,3},{6,5},{3,0},{7,6},{8,9},{12,15},{9,1... | collective-permute-start | bytes 1327112 | tf_op jit(solution)/shard_map/ppermute | solution.py:28
  78.5 2.4 %collective-permute-start.5 = (bf16[2,48,1536]{2,1,0:T(8,128)(2,1)S(1)}, bf16[2,48,1536]{2,1,0:T(8,128)(2,1)S(1)}, u32[]{:S(2)}, u32[]{:S(2)}) collective-permute-start(bf16[2,48,1536]{2,1,0:T(8,128)(2,1)S(1)} %constant_dynamic-update-slice_fusion.refs_0_), channel_id=1, source_target_pairs={{0,224},{32,0},{64,32},{96,64},{128,96},{160,128},{192,160},{224,1... | collective-permute-start | bytes 884744 | tf_op jit(solution)/shard_map/ppermute | solution.py:22
  80.9 2.2 %collective-permute-done.1.refs_1_ = bf16[2,48,1536]{2,1,0:T(8,128)(2,1)S(1)} collective-permute-done((bf16[2,48,1536]{2,1,0:T(8,128)(2,1)S(1)}, bf16[2,48,1536]{2,1,0:T(8,128)(2,1)S(1)}, u32[]{:S(2)}, u32[]{:S(2)}) %collective-permute-start.1) | collective-permute-done | bytes 294944 | tf_op jit(solution)/shard_map/ppermute | solution.py:22
  83.1 3.5 %collective-permute-start.2 = (bf16[2,48,1536]{2,1,0:T(8,128)(2,1)S(1)}, bf16[2,48,1536]{2,1,0:T(8,128)(2,1)S(1)}, u32[]{:S(2)}, u32[]{:S(2)}) collective-permute-start(bf16[2,48,1536]{2,1,0:T(8,128)(2,1)S(1)} %collective-permute-done.1.refs_1_), channel_id=1, source_target_pairs={{0,32},{32,64},{64,96},{96,128},{128,160},{160,192},{192,224},{224... | collective-permute-start | bytes 884744 | tf_op jit(solution)/shard_map/ppermute | solution.py:22
  86.6 2.5 %collective-permute-done.5.refs_4_ = bf16[2,48,1536]{2,1,0:T(8,128)(2,1)S(1)} collective-permute-done((bf16[2,48,1536]{2,1,0:T(8,128)(2,1)S(1)}, bf16[2,48,1536]{2,1,0:T(8,128)(2,1)S(1)}, u32[]{:S(2)}, u32[]{:S(2)}) %collective-permute-start.5) | collective-permute-done | bytes 294944 | tf_op jit(solution)/shard_map/ppermute | solution.py:22
  89.2 2.3 %collective-permute-start.6 = (bf16[2,48,1536]{2,1,0:T(8,128)(2,1)S(1)}, bf16[2,48,1536]{2,1,0:T(8,128)(2,1)S(1)}, u32[]{:S(2)}, u32[]{:S(2)}) collective-permute-start(bf16[2,48,1536]{2,1,0:T(8,128)(2,1)S(1)} %collective-permute-done.5.refs_4_), channel_id=1, source_target_pairs={{0,224},{32,0},{64,32},{96,64},{128,96},{160,128},{192,160},{224,1... | collective-permute-start | bytes 884744 | tf_op jit(solution)/shard_map/ppermute | solution.py:22
  91.5 2.1 %collective-permute-done.2.refs_2_ = bf16[2,48,1536]{2,1,0:T(8,128)(2,1)S(1)} collective-permute-done((bf16[2,48,1536]{2,1,0:T(8,128)(2,1)S(1)}, bf16[2,48,1536]{2,1,0:T(8,128)(2,1)S(1)}, u32[]{:S(2)}, u32[]{:S(2)}) %collective-permute-start.2) | collective-permute-done | bytes 294944 | tf_op jit(solution)/shard_map/ppermute | solution.py:22
  93.6 2.7 %collective-permute-start.3 = (bf16[2,48,1536]{2,1,0:T(8,128)(2,1)S(1)}, bf16[2,48,1536]{2,1,0:T(8,128)(2,1)S(1)}, u32[]{:S(2)}, u32[]{:S(2)}) collective-permute-start(bf16[2,48,1536]{2,1,0:T(8,128)(2,1)S(1)} %collective-permute-done.2.refs_2_), channel_id=1, source_target_pairs={{0,32},{32,64},{64,96},{96,128},{128,160},{160,192},{192,224},{224... | collective-permute-start | bytes 884744 | tf_op jit(solution)/shard_map/ppermute | solution.py:22
  96.3 2.5 %collective-permute-start.10 = (bf16[6,96,384]{2,1,0:T(8,128)(2,1)S(1)}, bf16[6,96,384]{2,1,0:T(8,128)(2,1)S(1)}, u32[]{:S(2)}, u32[]{:S(2)}) collective-permute-start(bf16[6,96,384]{2,1,0:T(8,128)(2,1)S(1)} %collective-permute-done.8.refs_6_.refs_4_), channel_id=1, source_target_pairs={{0,1},{4,7},{1,2},{5,4},{2,3},{6,5},{3,0},{7,6},{8,9},{12,15},{9,1... | collective-permute-start | bytes 1327112 | tf_op jit(solution)/shard_map/ppermute | solution.py:28
  98.8 1.9 %collective-permute-start.9 = (bf16[6,96,384]{2,1,0:T(8,128)(2,1)S(1)}, bf16[6,96,384]{2,1,0:T(8,128)(2,1)S(1)}, u32[]{:S(2)}, u32[]{:S(2)}) collective-permute-start(bf16[6,96,384]{2,1,0:T(8,128)(2,1)S(1)} %collective-permute-done.8.refs_6_.refs_4_), channel_id=1, source_target_pairs={{0,4},{4,0},{1,5},{5,1},{2,6},{6,2},{3,7},{7,3},{8,12},{12,8},{9,1... | collective-permute-start | bytes 1327112 | tf_op jit(solution)/shard_map/ppermute | solution.py:22
  100.8 4.0 %collective-permute-start.7 = (bf16[2,48,1536]{2,1,0:T(8,128)(2,1)S(1)}, bf16[2,48,1536]{2,1,0:T(8,128)(2,1)S(1)}, u32[]{:S(2)}, u32[]{:S(2)}) collective-permute-start(bf16[2,48,1536]{2,1,0:T(8,128)(2,1)S(1)} %collective-permute-done.6.refs_3_), channel_id=1, source_target_pairs={{0,224},{32,0},{64,32},{96,64},{128,96},{160,128},{192,160},{224,1... | collective-permute-start | bytes 884744 | tf_op jit(solution)/shard_map/ppermute | solution.py:22
  104.8 2.9 %collective-permute-start.4 = (bf16[2,48,1536]{2,1,0:T(8,128)(2,1)S(1)}, bf16[2,48,1536]{2,1,0:T(8,128)(2,1)S(1)}, u32[]{:S(2)}, u32[]{:S(2)}) collective-permute-start(bf16[2,48,1536]{2,1,0:T(8,128)(2,1)S(1)} %collective-permute-done.3.refs_0_), channel_id=1, source_target_pairs={{0,32},{32,64},{64,96},{96,128},{128,160},{160,192},{192,224},{224... | collective-permute-start | bytes 884744 | tf_op jit(solution)/shard_map/ppermute | solution.py:22
  107.7 0.0 collective-permute-done.10.refs_8_.refs_6_
  107.8 2.4 %shard_map.46.refs_7_ = bf16[16,288,96]{2,1,0:T(8,128)(2,1)S(1)} custom-call(s32[4,8]{1,0:T(4,128)S(1)} %bitcast.4, bf16[2,48,1536]{2,1,0:T(8,128)(2,1)S(1)} %constant_dynamic-update-slice_fusion.refs_0_, bf16[2,48,1536]{2,1,0:T(8,128)(2,1)S(1)} %collective-permute-done.1.refs_1_, bf16[2,48,1536]{2,1,0:T(8,128)(2,1)S(1)} %collective-permute-done.2.refs_2_, ...), custom_call_target="tpu_custom_call" | custom-call | tf_op jit(solution)/shard_map/pallas_call | solution.py:86
  110.2 3.3 %collective-permute-done.7.refs_2_ = bf16[2,48,1536]{2,1,0:T(8,128)(2,1)S(1)} collective-permute-done((bf16[2,48,1536]{2,1,0:T(8,128)(2,1)S(1)}, bf16[2,48,1536]{2,1,0:T(8,128)(2,1)S(1)}, u32[]{:S(2)}, u32[]{:S(2)}) %collective-permute-start.7) | collective-permute-done | bytes 294944 | tf_op jit(solution)/shard_map/ppermute | solution.py:22
  113.4 3.9 %collective-permute-done.4.refs_1_ = bf16[2,48,1536]{2,1,0:T(8,128)(2,1)S(1)} collective-permute-done((bf16[2,48,1536]{2,1,0:T(8,128)(2,1)S(1)}, bf16[2,48,1536]{2,1,0:T(8,128)(2,1)S(1)}, u32[]{:S(2)}, u32[]{:S(2)}) %collective-permute-start.4) | collective-permute-done | bytes 294944 | tf_op jit(solution)/shard_map/ppermute | solution.py:22
  117.3 1.9 %shard_map.47.half = bf16[16,288,96]{2,1,0:T(8,128)(2,1)S(1)} custom-call(s32[4,8]{1,0:T(4,128)S(1)} %bitcast.5, bf16[2,48,1536]{2,1,0:T(8,128)(2,1)S(1)} %collective-permute-done.3.refs_0_, bf16[2,48,1536]{2,1,0:T(8,128)(2,1)S(1)} %collective-permute-done.4.refs_1_, bf16[2,48,1536]{2,1,0:T(8,128)(2,1)S(1)} %collective-permute-done.7.refs_2_, ...), custom_call_target="tpu_custom_call" | custom-call | tf_op jit(solution)/shard_map/pallas_call | solution.py:86
  119.2 2.5 %total.1 = bf16[16,216,128]{2,1,0:T(8,128)(2,1)S(1)} custom-call(bf16[16,288,96]{2,1,0:T(8,128)(2,1)S(1)} %shard_map.47.half, bf16[4,4,2,96,384]{4,3,2,1,0:T(8,128)(2,1)S(1)} %all_to_all.16.mine, bf16[4,4,2,96,384]{4,3,2,1,0:T(8,128)(2,1)S(1)} %collective-permute-done.11.theirs), custom_call_target="tpu_custom_call" | custom-call | tf_op jit(solution)/shard_map/total/pallas_call | solution.py:155
  121.7 40.2 %all_to_all.17.parts = bf16[16,216,128]{2,1,0:T(8,128)(2,1)S(1)} all-to-all(bf16[16,216,128]{2,1,0:T(8,128)(2,1)S(1)} %total.1), channel_id=1, replica_groups=mesh['zh'=2,'y'=8,'zl'=4,'core'=2,'x'=4] {'zh','y'}, dimensions={0} | all-to-all | bytes 1769472 | tf_op jit(solution)/shard_map/all_to_all | solution.py:164
  162.0 0.8 sum.1
  (12 shorter events, 0.1 us)
Async XLA Ops:
  0.0 1.1 copy-start
  22.4 34.1 %copy-start.3 = (bf16[1,48,1536]{2,1,0:T(8,128)(2,1)S(1)}, bf16[1,48,1536]{2,1,0:T(8,128)(2,1)}, u32[]{:S(2)}) copy-start(bf16[1,48,1536]{2,1,0:T(8,128)(2,1)} %param.6) | copy-start | bytes 442372
  22.5 53.6 %copy-start.1 = (bf16[6,96,384]{2,1,0:T(8,128)(2,1)S(1)}, bf16[6,96,384]{2,1,0:T(8,128)(2,1)}, u32[]{:S(2)}) copy-start(bf16[6,96,384]{2,1,0:T(8,128)(2,1)} %refs_3_.1) | copy-start | bytes 1327108
  22.5 85.3 %copy-start.2 = (s32[8,4]{0,1:T(4,128)S(1)}, s32[8,4]{0,1:T(4,128)}, u32[]{:S(2)}) copy-start(s32[8,4]{0,1:T(4,128)} %param.7) | copy-start | bytes 388
  54.6 64.6 %collective-permute-start.11 = (bf16[4,4,2,96,384]{4,3,2,1,0:T(8,128)(2,1)S(1)}, bf16[4,4,2,96,384]{4,3,2,1,0:T(8,128)(2,1)S(1)}, u32[]{:S(2)}, u32[]{:S(2)}) collective-permute-start(bf16[4,4,2,96,384]{4,3,2,1,0:T(8,128)(2,1)S(1)} %all_to_all.16.mine), channel_id=1, source_target_pairs={{0,4},{4,0},{1,5},{5,1},{2,6},{6,2},{3,7},{7,3},{8,12},{12,8},{9,1... | collective-permute-start | bytes 7077896 | tf_op jit(solution)/shard_map/ppermute | solution.py:22
  56.5 16.0 %collective-permute-start = (bf16[1,48,1536]{2,1,0:T(8,128)(2,1)S(1)}, bf16[1,48,1536]{2,1,0:T(8,128)(2,1)S(1)}, u32[]{:S(2)}, u32[]{:S(2)}) collective-permute-start(bf16[1,48,1536]{2,1,0:T(8,128)(2,1)S(1)} %copy-done.3), channel_id=1, source_target_pairs={{0,256},{256,0},{1,257},{257,1},{2,258},{258,2},{3,259},{259,3},{4... | collective-permute-start | bytes 442376 | tf_op jit(solution)/shard_map/ppermute | solution.py:22
  72.6 10.6 %collective-permute-start.1 = (bf16[2,48,1536]{2,1,0:T(8,128)(2,1)S(1)}, bf16[2,48,1536]{2,1,0:T(8,128)(2,1)S(1)}, u32[]{:S(2)}, u32[]{:S(2)}) collective-permute-start(bf16[2,48,1536]{2,1,0:T(8,128)(2,1)S(1)} %constant_dynamic-update-slice_fusion.refs_0_), channel_id=1, source_target_pairs={{0,32},{32,64},{64,96},{96,128},{128,160},{160,192},{192,224},{224... | collective-permute-start | bytes 884744 | tf_op jit(solution)/shard_map/ppermute | solution.py:22
  76.1 20.3 %collective-permute-start.8 = (bf16[6,96,384]{2,1,0:T(8,128)(2,1)S(1)}, bf16[6,96,384]{2,1,0:T(8,128)(2,1)S(1)}, u32[]{:S(2)}, u32[]{:S(2)}) collective-permute-start(bf16[6,96,384]{2,1,0:T(8,128)(2,1)S(1)} %copy-done.1), channel_id=1, source_target_pairs={{0,1},{4,7},{1,2},{5,4},{2,3},{6,5},{3,0},{7,6},{8,9},{12,15},{9,1... | collective-permute-start | bytes 1327112 | tf_op jit(solution)/shard_map/ppermute | solution.py:28
  78.5 10.6 %collective-permute-start.5 = (bf16[2,48,1536]{2,1,0:T(8,128)(2,1)S(1)}, bf16[2,48,1536]{2,1,0:T(8,128)(2,1)S(1)}, u32[]{:S(2)}, u32[]{:S(2)}) collective-permute-start(bf16[2,48,1536]{2,1,0:T(8,128)(2,1)S(1)} %constant_dynamic-update-slice_fusion.refs_0_), channel_id=1, source_target_pairs={{0,224},{32,0},{64,32},{96,64},{128,96},{160,128},{192,160},{224,1... | collective-permute-start | bytes 884744 | tf_op jit(solution)/shard_map/ppermute | solution.py:22
  83.1 10.4 %collective-permute-start.2 = (bf16[2,48,1536]{2,1,0:T(8,128)(2,1)S(1)}, bf16[2,48,1536]{2,1,0:T(8,128)(2,1)S(1)}, u32[]{:S(2)}, u32[]{:S(2)}) collective-permute-start(bf16[2,48,1536]{2,1,0:T(8,128)(2,1)S(1)} %collective-permute-done.1.refs_1_), channel_id=1, source_target_pairs={{0,32},{32,64},{64,96},{96,128},{128,160},{160,192},{192,224},{224... | collective-permute-start | bytes 884744 | tf_op jit(solution)/shard_map/ppermute | solution.py:22
  89.2 11.6 %collective-permute-start.6 = (bf16[2,48,1536]{2,1,0:T(8,128)(2,1)S(1)}, bf16[2,48,1536]{2,1,0:T(8,128)(2,1)S(1)}, u32[]{:S(2)}, u32[]{:S(2)}) collective-permute-start(bf16[2,48,1536]{2,1,0:T(8,128)(2,1)S(1)} %collective-permute-done.5.refs_4_), channel_id=1, source_target_pairs={{0,224},{32,0},{64,32},{96,64},{128,96},{160,128},{192,160},{224,1... | collective-permute-start | bytes 884744 | tf_op jit(solution)/shard_map/ppermute | solution.py:22
  93.6 11.2 %collective-permute-start.3 = (bf16[2,48,1536]{2,1,0:T(8,128)(2,1)S(1)}, bf16[2,48,1536]{2,1,0:T(8,128)(2,1)S(1)}, u32[]{:S(2)}, u32[]{:S(2)}) collective-permute-start(bf16[2,48,1536]{2,1,0:T(8,128)(2,1)S(1)} %collective-permute-done.2.refs_2_), channel_id=1, source_target_pairs={{0,32},{32,64},{64,96},{96,128},{128,160},{160,192},{192,224},{224... | collective-permute-start | bytes 884744 | tf_op jit(solution)/shard_map/ppermute | solution.py:22
  96.3 11.4 %collective-permute-start.10 = (bf16[6,96,384]{2,1,0:T(8,128)(2,1)S(1)}, bf16[6,96,384]{2,1,0:T(8,128)(2,1)S(1)}, u32[]{:S(2)}, u32[]{:S(2)}) collective-permute-start(bf16[6,96,384]{2,1,0:T(8,128)(2,1)S(1)} %collective-permute-done.8.refs_6_.refs_4_), channel_id=1, source_target_pairs={{0,1},{4,7},{1,2},{5,4},{2,3},{6,5},{3,0},{7,6},{8,9},{12,15},{9,1... | collective-permute-start | bytes 1327112 | tf_op jit(solution)/shard_map/ppermute | solution.py:28
  98.8 8.9 %collective-permute-start.9 = (bf16[6,96,384]{2,1,0:T(8,128)(2,1)S(1)}, bf16[6,96,384]{2,1,0:T(8,128)(2,1)S(1)}, u32[]{:S(2)}, u32[]{:S(2)}) collective-permute-start(bf16[6,96,384]{2,1,0:T(8,128)(2,1)S(1)} %collective-permute-done.8.refs_6_.refs_4_), channel_id=1, source_target_pairs={{0,4},{4,0},{1,5},{5,1},{2,6},{6,2},{3,7},{7,3},{8,12},{12,8},{9,1... | collective-permute-start | bytes 1327112 | tf_op jit(solution)/shard_map/ppermute | solution.py:22
  100.8 12.7 %collective-permute-start.7 = (bf16[2,48,1536]{2,1,0:T(8,128)(2,1)S(1)}, bf16[2,48,1536]{2,1,0:T(8,128)(2,1)S(1)}, u32[]{:S(2)}, u32[]{:S(2)}) collective-permute-start(bf16[2,48,1536]{2,1,0:T(8,128)(2,1)S(1)} %collective-permute-done.6.refs_3_), channel_id=1, source_target_pairs={{0,224},{32,0},{64,32},{96,64},{128,96},{160,128},{192,160},{224,1... | collective-permute-start | bytes 884744 | tf_op jit(solution)/shard_map/ppermute | solution.py:22
  104.8 12.5 %collective-permute-start.4 = (bf16[2,48,1536]{2,1,0:T(8,128)(2,1)S(1)}, bf16[2,48,1536]{2,1,0:T(8,128)(2,1)S(1)}, u32[]{:S(2)}, u32[]{:S(2)}) collective-permute-start(bf16[2,48,1536]{2,1,0:T(8,128)(2,1)S(1)} %collective-permute-done.3.refs_0_), channel_id=1, source_target_pairs={{0,32},{32,64},{64,96},{96,128},{128,160},{160,192},{192,224},{224... | collective-permute-start | bytes 884744 | tf_op jit(solution)/shard_map/ppermute | solution.py:22
